TPU v7x, 32 devices: a whole 2x2x4 slice. The times are simulated.
32 devices in a mesh: blk: 16 (over z, y, x), obs: 2 (over core).
Axes of the slice: x: 2, y: 2, z: 4, core: 2. Of those that a mesh axis runs over, the one named last changes fastest.
Arguments:
- populations: float32 [16, 19, 32, 1024], P('blk', None, 'obs'), may hold values from 0.011111111 to 0.533333333, as said below
- block_faces: int32 [16, 4], P('blk'), may hold values from 0 to 15, as said below
- block_edges: int32 [16, 4], P('blk'), may hold values from 0 to 15, as said below
- probe_cell: int32 [4096], P(('blk', 'obs')), may hold values from 0 to 16383
- history: bfloat16 [4096, 512], P(('blk', 'obs')), may hold values from -6 to 6
- panel_count: int32 [32], P(('blk', 'obs')), may hold values from 0 to 128, as said below
- panel_owner: int32 [4096], P(('blk', 'obs')), may hold values from 0 to 1023, as said below
- panel_pos: bfloat16 [3, 2048], P(None, ('blk', 'obs')), may hold values from -1 to 1
- panel_normal: bfloat16 [3, 2048], P(None, ('blk', 'obs')), may hold values from -0.625 to 0.625
- observers: float32 [3, 1024], P(None, 'obs'), may hold values from -8 to 8, as said below
Outputs:
- populations_out: float32 [16, 19, 32, 1024], P('blk', None, 'obs')
- spectrum: float32 [2, 512, 128], P('obs', 'blk')
Inputs may be any that keep to these rules, and one draw needn't show every extreme that they name: `populations`: every population is positive. The blocks form a lattice of 4 by 4 blocks along y and z, periodic in both, one block deep in x; block_faces[b] names the blocks beside b at -y, +y, -z, +z. block_edges[b] names the blocks at (-y,-z), (-y,+z), (+y,-z), (+y,+z) of b: the y neighbour's z neighbour, which is the z neighbour's y neighbour. The eight face and edge neighbours of a block are distinct and differ from it. The live slots of a device are its first panel_count slots. The counts of the devices at one obs index sum to 1024. `panel_owner`: in a live slot of the device at blk index b and obs index o the value is q * 64 + j: slot j of the owner at blk index q and the same obs index. Every owner slot receives exactly one live panel. A device sends at most 8 live panels to one owner, and its live panels go to the owners in numbers that differ by at most one. Dead slots hold arbitrary values of the range. `observers`: every observer lies at a distance of 4 to 8 from the anchor (0, 0, 0).
All inputs are finite; a program needn't handle non-finite values.
Results may differ from a plain program's by a relative error of at most 0.0032.
The roundings to bfloat16 on the way count: a program that leaves them out, or rounds other values in their place, can miss the bound.
Values may be sent and summed in bfloat16 or wider, within the bound.
A program may use at most 128 MiB of HBM per device.

v0:
```python
import math
import jax
import jax.numpy as jnp
from jax import lax
from jax.sharding import PartitionSpec as P

BS = 32
STEPS = 4
SAMPLES = 256
BINS = 64
P_OWN = 64
velocity_list = [
    (0, 0, 0),
    (1, 0, 0),
    (-1, 0, 0),
    (0, 1, 0),
    (0, -1, 0),
    (0, 0, 1),
    (0, 0, -1),
    (1, 1, 0),
    (-1, -1, 0),
    (1, -1, 0),
    (-1, 1, 0),
    (1, 0, 1),
    (-1, 0, -1),
    (1, 0, -1),
    (-1, 0, 1),
    (0, 1, 1),
    (0, -1, -1),
    (0, 1, -1),
    (0, -1, 1),
]
weight_list = [1.0 / 3.0] + [1.0 / 18.0] * 6 + [1.0 / 36.0] * 12
x_moving = [1, 2, 7, 8, 9, 10, 11, 12, 13, 14]
y_upward = [3, 7, 10, 15, 17]
y_downward = [4, 8, 9, 16, 18]
z_upward = [5, 11, 14, 15, 18]
z_downward = [6, 12, 13, 16, 17]
relax_rate = 1.6
pressure_gain = 60.0
sound_speed = 0.5


def padded(block, sides, width):
    for axis, dim in sides:
        count = lax.axis_size(axis)
        forward = [(i, i + 1) for i in range(count - 1)]
        forward.append((count - 1, 0))
        backward = [(target, source) for source, target in forward]
        low = lax.ppermute(
            lax.slice_in_dim(block, block.shape[dim] - width, None, axis=dim), axis, forward
        )
        high = lax.ppermute(lax.slice_in_dim(block, 0, width, axis=dim), axis, backward)
        block = jnp.concatenate([low, block, high], axis=dim)
    return block


def component(axis_number, extra):
    values = jnp.array([velocity[axis_number] for velocity in velocity_list], jnp.float32)
    return values.reshape((19,) + extra)


def collide(field):
    extra = (1,) * (field.ndim - 1)
    along_x = component(0, extra)
    along_y = component(1, extra)
    along_z = component(2, extra)
    weights = jnp.array(weight_list, jnp.float32).reshape((19,) + extra)
    density = jnp.sum(field, axis=0)
    speed_x = jnp.sum(along_x * field, axis=0) / density
    speed_y = jnp.sum(along_y * field, axis=0) / density
    speed_z = jnp.sum(along_z * field, axis=0) / density
    projected = along_x * speed_x + along_y * speed_y + along_z * speed_z
    squared = speed_x * speed_x + speed_y * speed_y + speed_z * speed_z
    equilibrium = (
        weights * density * (1.0 + 3.0 * projected + 4.5 * projected * projected - 1.5 * squared)
    )
    return field + relax_rate * (equilibrium - field)


def stream_merged(widened, planes):
    below_plane, above_plane, near_plane, far_plane = planes
    slab_depth = widened.shape[1] - 2
    lane_count = widened.shape[2]
    lane_index = jnp.arange(lane_count, dtype=jnp.int32)
    lane_row = lane_index // BS
    lane_column = lane_index % BS
    parts = []
    for number, velocity in enumerate(velocity_list):
        shift_x, shift_y, shift_z = velocity
        begin = 1 - shift_x
        moved = jnp.roll(
            widened[number, begin : begin + slab_depth], shift_y * BS + shift_z, axis=-1
        )
        if shift_y != 0:
            source_plane = below_plane if shift_y == 1 else above_plane
            row_values = jnp.roll(
                source_plane[number, begin : begin + slab_depth], shift_z, axis=-1
            )
            edge_index = 0 if shift_y == 1 else BS - 1
            moved = jnp.where(
                (lane_row == edge_index)[None, :], jnp.tile(row_values, (1, BS)), moved
            )
        if shift_z != 0:
            source_plane = near_plane if shift_z == 1 else far_plane
            column_values = source_plane[
                number, begin : begin + slab_depth, 1 - shift_y : 1 - shift_y + BS
            ]
            edge_index = 0 if shift_z == 1 else BS - 1
            moved = jnp.where(
                (lane_column == edge_index)[None, :], jnp.repeat(column_values, BS, axis=-1), moved
            )
        parts.append(moved)
    return jnp.stack(parts)


def place_pieces(pieces, targets, blocks):
    onehot = (targets[:, None] == jnp.arange(blocks, dtype=jnp.int32)[None, :]).astype(jnp.float32)
    return jnp.einsum("kn,kf->nf", onehot, pieces, precision=lax.Precision.HIGHEST)


def spread_pops(piece, chosen, shape):
    return jnp.zeros(shape, jnp.float32).at[jnp.array(chosen)].set(piece)


def direct_halo(widened, block_faces, block_edges, blocks):
    depth_x = widened.shape[1]
    lane_count = widened.shape[2]

    def corner_piece(number, lane_at):
        return jnp.zeros((5, depth_x, BS), jnp.float32).at[0, :, 0].set(widened[number, :, lane_at])

    def corner_plane(number, vector):
        return jnp.zeros((19, depth_x, 1), jnp.float32).at[number, :, 0].set(vector)

    outgoing = jnp.stack(
        [
            widened[jnp.array(y_downward), :, 0:BS],
            widened[jnp.array(y_upward), :, lane_count - BS :],
            widened[jnp.array(z_downward), :, 0::BS],
            widened[jnp.array(z_upward), :, BS - 1 :: BS],
            corner_piece(16, 0),
            corner_piece(18, BS - 1),
            corner_piece(17, (BS - 1) * BS),
            corner_piece(15, BS * BS - 1),
        ]
    ).reshape(8, -1)
    targets = jnp.concatenate([block_faces, block_edges])
    received = lax.all_to_all(
        place_pieces(outgoing, targets, blocks), "blk", split_axis=0, concat_axis=0, tiled=True
    )
    chosen = jnp.take(received, targets, axis=0).reshape(8, 5, depth_x, BS)
    below_plane = spread_pops(chosen[0], y_upward, (19, depth_x, BS))
    above_plane = spread_pops(chosen[1], y_downward, (19, depth_x, BS))
    near_core = spread_pops(chosen[2], z_upward, (19, depth_x, BS))
    far_core = spread_pops(chosen[3], z_downward, (19, depth_x, BS))
    near_plane = jnp.concatenate(
        [corner_plane(15, chosen[4, 0, :, 0]), near_core, corner_plane(18, chosen[6, 0, :, 0])],
        axis=2,
    )
    far_plane = jnp.concatenate(
        [corner_plane(17, chosen[5, 0, :, 0]), far_core, corner_plane(16, chosen[7, 0, :, 0])],
        axis=2,
    )
    return (below_plane, above_plane, near_plane, far_plane)


def transform_table():
    moments = jnp.arange(SAMPLES, dtype=jnp.int32)[:, None]
    harmonics = jnp.arange(BINS, dtype=jnp.int32)[None, :] + 1
    turns = moments * harmonics % SAMPLES
    phases = turns.astype(jnp.float32) * (2.0 * math.pi / SAMPLES)
    return jnp.concatenate([jnp.cos(phases), -jnp.sin(phases)], axis=1).astype(jnp.bfloat16)


def radiate(spectra, place, normal, listen):
    values = spectra.astype(jnp.float32)
    press_real = values[0:BINS].T
    press_imag = values[BINS : 2 * BINS].T
    rate_real = values[2 * BINS : 3 * BINS].T
    rate_imag = values[3 * BINS : 4 * BINS].T
    offsets = listen[:, None, :] - place.astype(jnp.float32)[:, :, None]
    distance_sq = jnp.sum(offsets * offsets, axis=0)
    distance = jnp.sqrt(distance_sq)
    facing = jnp.sum(normal.astype(jnp.float32)[:, :, None] * offsets, axis=0)
    far_term = facing / (4.0 * math.pi * sound_speed * distance_sq)
    near_term = facing / (4.0 * math.pi * distance_sq * distance)
    angular = (jnp.arange(BINS, dtype=jnp.float32) + 1.0) * (2.0 * math.pi / SAMPLES)
    phases = angular[None, :, None] * (distance / sound_speed)[:, None, :]
    cosine = jnp.cos(phases)
    sine_part = jnp.sin(phases)
    weight_real = (
        far_term[:, None, :] * rate_real[:, :, None]
        + near_term[:, None, :] * press_real[:, :, None]
    )
    weight_imag = (
        far_term[:, None, :] * rate_imag[:, :, None]
        + near_term[:, None, :] * press_imag[:, :, None]
    )
    real_part = jnp.sum(weight_real * cosine + weight_imag * sine_part, axis=0)
    imag_part = jnp.sum(weight_imag * cosine - weight_real * sine_part, axis=0)
    return jnp.concatenate([real_part, imag_part], axis=0).T


def radiate_blocks(spectra, place, normal, listen):
    count_panels = spectra.shape[1]
    listener_count = listen.shape[1]
    block_size = 128
    while block_size > 1 and (
        count_panels % block_size != 0 or block_size * listener_count > 16384
    ):
        block_size = block_size // 2

    def radiate_accumulate(block_number, total):
        begin = block_number * block_size
        return total + radiate(
            lax.dynamic_slice_in_dim(spectra, begin, block_size, 1),
            lax.dynamic_slice_in_dim(place, begin, block_size, 1),
            lax.dynamic_slice_in_dim(normal, begin, block_size, 1),
            listen,
        )

    return lax.fori_loop(
        0,
        count_panels // block_size,
        radiate_accumulate,
        jnp.zeros((listener_count, 2 * BINS), jnp.float32),
    )


def route_slots(payload, owners, alive_slot, blocks):
    count_slots = payload.shape[0]
    capacity = -(-count_slots // blocks)
    target = owners // P_OWN
    member = (
        (target[:, None] == jnp.arange(blocks, dtype=jnp.int32)[None, :]) & alive_slot[:, None]
    ).astype(jnp.int32)
    before = jnp.cumsum(member, axis=0) - member
    order_within = jnp.sum(before * member, axis=1)
    slot_label = jnp.where(alive_slot, target * capacity + order_within, -1)
    matches = slot_label[:, None] == jnp.arange(blocks * capacity, dtype=jnp.int32)[None, :]
    source = jnp.sum(
        jnp.where(matches, jnp.arange(count_slots, dtype=jnp.int32)[:, None], 0), axis=0
    )
    filled = jnp.any(matches, axis=0)
    outgoing = jnp.take(payload, source, axis=0).reshape(blocks, capacity, payload.shape[1])
    tagged = jnp.where(filled, jnp.take(owners, source), -1).reshape(blocks, capacity)
    return (outgoing, tagged)


def settle(incoming, tagged):
    keeper = lax.axis_index("blk")
    flat_tags = tagged.reshape(-1)
    slot_here = flat_tags - keeper * P_OWN
    choose = (
        (slot_here[:, None] == jnp.arange(P_OWN, dtype=jnp.int32)[None, :])
        & (flat_tags[:, None] >= 0)
    ).astype(jnp.bfloat16)
    return jnp.einsum(
        "rw,rp->wp",
        incoming.reshape(-1, incoming.shape[-1]),
        choose,
        preferred_element_type=jnp.float32,
    ).astype(jnp.bfloat16)


def body(
    populations,
    block_faces,
    block_edges,
    probe_cell,
    history,
    panel_count,
    panel_owner,
    panel_pos,
    panel_normal,
    observers,
):
    blocks = lax.axis_size("blk")
    lattice_state = populations[0]
    slab_depth = lattice_state.shape[1]
    lane_count = lattice_state.shape[2]
    faces_here = block_faces[0]
    edges_here = block_edges[0]
    readings = []
    for turn_index in range(STEPS):
        collided = collide(lattice_state)
        slab_edges = padded(collided[jnp.array(x_moving)], (("obs", 1),), 1)
        lower_plane = spread_pops(slab_edges[:, 0:1], x_moving, (19, 1, lane_count))
        upper_plane = spread_pops(slab_edges[:, -1:], x_moving, (19, 1, lane_count))
        widened = jnp.concatenate([lower_plane, collided, upper_plane], axis=1)
        planes = direct_halo(widened, faces_here, edges_here, blocks)
        lattice_state = stream_merged(widened, planes)
        density = jnp.sum(lattice_state, axis=0).reshape(-1)
        readings.append(jnp.take(density, probe_cell))
    populations_out = lattice_state.reshape(1, 19, slab_depth, lane_count)
    gained = pressure_gain * (jnp.stack(readings, axis=1) - 1.0)
    previous = jnp.concatenate(
        [history[:, SAMPLES - 1 : SAMPLES].astype(jnp.float32), gained[:, :-1]], axis=1
    )
    rate_values = gained - previous
    recent = jnp.concatenate(
        [
            history[:, STEPS:SAMPLES],
            gained.astype(jnp.bfloat16),
            history[:, SAMPLES + STEPS :],
            rate_values.astype(jnp.bfloat16),
        ],
        axis=1,
    )
    transform = transform_table()
    count_slots = recent.shape[0]
    alive_slot = jnp.arange(count_slots, dtype=jnp.int32) < panel_count[0]
    outgoing, tagged = route_slots(recent, panel_owner, alive_slot, blocks)
    incoming, tags_in = (
        lax.all_to_all(outgoing, "blk", split_axis=0, concat_axis=0, tiled=True),
        lax.all_to_all(tagged, "blk", split_axis=0, concat_axis=0, tiled=True),
    )
    histories = settle(incoming, tags_in).reshape(2, SAMPLES, P_OWN)
    spectra = (
        jnp.einsum("tk,gtp->gkp", transform, histories, preferred_element_type=jnp.float32)
        .astype(jnp.bfloat16)
        .reshape(4 * BINS, P_OWN)
    )
    partial_value = radiate_blocks(
        lax.all_gather(spectra, "obs", axis=1, tiled=True),
        lax.all_gather(panel_pos, "obs", axis=1, tiled=True),
        lax.all_gather(panel_normal, "obs", axis=1, tiled=True),
        observers,
    )
    summed = lax.psum_scatter(partial_value, "blk", scatter_dimension=0, tiled=True)
    return (populations_out, summed.reshape(1, -1, 2 * BINS))


def solution(mesh):
    placed = (
        P("blk", None, "obs", None),
        P("blk", None),
        P("blk", None),
        P(("blk", "obs")),
        P(("blk", "obs"), None),
        P(("blk", "obs")),
        P(("blk", "obs")),
        P(None, ("blk", "obs")),
        P(None, ("blk", "obs")),
        P(None, "obs"),
    )
    return jax.shard_map(
        body,
        mesh=mesh,
        in_specs=placed,
        out_specs=(P("blk", None, "obs", None), P("obs", "blk", None)),
        check_vma=False,
    )
```

profile of v0, /device:TPU:0, one launch (start us, length us, event | category | flops | bytes accessed | tf_op | source)
XLA Modules:
  0.0 673.8 jit_solution(10351201009113472713)
XLA Ops:
  8.0 1.4 reduce_sum.891
  10.0 1.3 fusion.16
  16.9 1.2 gather_fusion.21
  21.0 1.9 all-gather.1
  23.0 1.8 all-gather
  56.1 5.3 copy.672
  61.4 7.4 %copy.668 = f32[19,18,1024]{1,0,2:T(8,128)} copy(f32[19,18,1024]{2,1,0:T(8,128)S(1)} %pad_maximum_fusion) | data formatting | bytes 2801664 | tf_op jit(solution)/shard_map/concatenate | solution.py:291
  69.6 2.7 gather_fusion.4
  72.3 2.7 gather_fusion.3
  75.5 1.5 gather_fusion.2
  77.1 1.5 gather_fusion.1
  80.6 8.4 %all-to-all-start = ((f32[16,1,2880]{2,1,0:T(1,128)}), f32[16,1,2880]{2,1,0:T(1,128)S(1)}, u32[]{:S(2)}, u32[]{:S(2)}) async-start(f32[16,1,2880]{2,1,0:T(1,128)} %copy.680), calls=%async_computation | async-start | bytes 376832 | tf_op jit(solution)/shard_map/all_to_all | solution.py:149
  138.1 1.0 constant_dynamic-update-slice_fusion.15
  141.1 1.0 constant_dynamic-update-slice_fusion.12
  151.6 1.3 fusion.22
  155.4 1.6 select_add_fusion.3
  157.0 1.3 gather_fusion.26
  159.7 1.0 scatter_custom_fusion.6
  184.0 5.2 copy.695
  189.2 3.4 gather_fusion.9
  192.6 3.4 gather_fusion.8
  196.0 7.4 %copy.691 = f32[19,18,1024]{1,0,2:T(8,128)} copy(f32[19,18,1024]{2,1,0:T(8,128)S(1)} %pad_maximum_fusion.1) | data formatting | bytes 2801664 | tf_op jit(solution)/shard_map/concatenate | solution.py:291
  203.4 1.5 gather_fusion.7
  204.9 1.5 gather_fusion.6
  209.7 7.3 %all-to-all-start.1 = ((f32[16,1,2880]{2,1,0:T(1,128)}), f32[16,1,2880]{2,1,0:T(1,128)S(1)}, u32[]{:S(2)}, u32[]{:S(2)}) async-start(f32[16,1,2880]{2,1,0:T(1,128)} %copy.703), calls=%async_computation.1 | async-start | bytes 376832 | tf_op jit(solution)/shard_map/all_to_all | solution.py:149
  269.4 1.0 constant_dynamic-update-slice_fusion.31
  279.8 1.3 fusion.28
  283.6 1.6 select_add_fusion.2
  285.2 1.8 gather_fusion.27
  312.2 5.2 copy.718
  317.4 3.4 gather_fusion.14
  320.8 3.4 gather_fusion.13
  324.2 7.4 %copy.714 = f32[19,18,1024]{1,0,2:T(8,128)} copy(f32[19,18,1024]{2,1,0:T(8,128)S(1)} %pad_maximum_fusion.2) | data formatting | bytes 2801664 | tf_op jit(solution)/shard_map/concatenate | solution.py:291
  331.6 1.5 gather_fusion.12
  333.1 1.5 gather_fusion.11
  337.9 7.1 %all-to-all-start.2 = ((f32[16,1,2880]{2,1,0:T(1,128)}), f32[16,1,2880]{2,1,0:T(1,128)S(1)}, u32[]{:S(2)}, u32[]{:S(2)}) async-start(f32[16,1,2880]{2,1,0:T(1,128)} %copy.726), calls=%async_computation.2 | async-start | bytes 376832 | tf_op jit(solution)/shard_map/all_to_all | solution.py:149
  397.4 1.0 constant_dynamic-update-slice_fusion.50
  407.8 1.3 fusion.34
  411.6 1.6 select_add_fusion.1
  413.2 1.9 gather_fusion.28
  415.9 1.1 scatter_custom_fusion.18
  429.7 5.2 copy.741
  434.9 2.7 gather_fusion.19
  437.7 2.7 gather_fusion.18
  440.4 7.4 %copy.737 = f32[19,18,1024]{1,0,2:T(8,128)} copy(f32[19,18,1024]{2,1,0:T(8,128)S(1)} %pad_maximum_fusion.3) | data formatting | bytes 2801664 | tf_op jit(solution)/shard_map/concatenate | solution.py:291
  447.8 1.5 gather_fusion.17
  449.3 1.5 gather_fusion.16
  453.9 6.9 %all-to-all-start.3 = ((f32[16,1,2880]{2,1,0:T(1,128)}), f32[16,1,2880]{2,1,0:T(1,128)S(1)}, u32[]{:S(2)}, u32[]{:S(2)}) async-start(f32[16,1,2880]{2,1,0:T(1,128)} %copy.749), calls=%async_computation.3 | async-start | bytes 376832 | tf_op jit(solution)/shard_map/all_to_all | solution.py:149
  463.5 5.7 all-to-all-done.3
  469.3 4.1 all-to-all-start.5
  485.5 1.6 fusion.114
  487.1 1.6 fusion.113
  489.5 1.6 fusion.111
  491.2 1.6 fusion.110
  501.5 1.3 gather_fusion.29
  505.0 7.0 %all-to-all-start.4 = ((bf16[16,8,512]{2,1,0:T(8,128)(2,1)}), bf16[16,8,512]{2,1,0:T(8,128)(2,1)S(1)}, u32[]{:S(2)}, u32[]{:S(2)}) async-start(bf16[16,8,512]{2,1,0:T(8,128)(2,1)} %bitcast_select_fusion), calls=%async_computation.4 | async-start | bytes 262144 | tf_op jit(solution)/shard_map/all_to_all | solution.py:316
  512.3 7.5 %all-to-all-done.4 = bf16[16,8,512]{2,1,0:T(8,128)(2,1)S(1)} async-done(((bf16[16,8,512]{2,1,0:T(8,128)(2,1)}), bf16[16,8,512]{2,1,0:T(8,128)(2,1)S(1)}, u32[]{:S(2)}, u32[]{:S(2)}) %all-to-all-start.4) | async-done | bytes 131104 | tf_op jit(solution)/shard_map/all_to_all | solution.py:316
  520.3 2.0 all_gather.11
  522.3 69.2 %while.46 = (s32[]{:T(128)}, f32[512,128]{0,1:T(8,128)S(1)}, bf16[3,128]{1,0:T(4,128)(2,1)S(1)}, f32[3,512]{1,0:T(4,128)S(1)}, bf16[3,128]{1,0:T(4,128)(2,1)S(1)...) while((s32[]{:T(128)}, f32[512,128]{0,1:T(8,128)S(1)}, ...), condition=%wide.region_46.49_spmd.clone, body=%wide.region_41.48_spmd.clone.sunk | while | flops 16179527 | bytes 1860141 | solution.py:223
  522.7 16.8 %fusion.295 = (f32[64,512]{1,0:T(8,128)S(1)}, f32[64,512]{1,0:T(8,128)S(1)}) fusion(f32[32,64]{1,0:T(8,128)S(1)} %get-tuple-element.1175, f32[32,64]{1,0:T(8,128)S(1)} %get-tuple-element.1176, f32[32,512]{1,0:T(8,128)S(1)} %get-tuple-element.1181, f32[64]{0:T(128)S(1)} %add_multiply_fusion.3, f32[32,64]{1,0:T(8,128)S(1)} %get-tuple-element.1182, ...), kind=kLoop, calls=%fused_computation.61.clone.1 | loop fusion | flops 15663104 | bytes 491776 | tf_op jit(solution)/shard_map/while/body/eval_jaxpr/reduce_sum | solution.py:200
  540.0 16.8 %fusion.295 = (f32[64,512]{1,0:T(8,128)S(1)}, f32[64,512]{1,0:T(8,128)S(1)}) fusion(f32[32,64]{1,0:T(8,128)S(1)} %get-tuple-element.1175, f32[32,64]{1,0:T(8,128)S(1)} %get-tuple-element.1176, f32[32,512]{1,0:T(8,128)S(1)} %get-tuple-element.1181, f32[64]{0:T(128)S(1)} %add_multiply_fusion.3, f32[32,64]{1,0:T(8,128)S(1)} %get-tuple-element.1182, ...), kind=kLoop, calls=%fused_computation.61.clone.1 | loop fusion | flops 15663104 | bytes 491776 | tf_op jit(solution)/shard_map/while/body/eval_jaxpr/reduce_sum | solution.py:200
  557.3 16.8 %fusion.295 = (f32[64,512]{1,0:T(8,128)S(1)}, f32[64,512]{1,0:T(8,128)S(1)}) fusion(f32[32,64]{1,0:T(8,128)S(1)} %get-tuple-element.1175, f32[32,64]{1,0:T(8,128)S(1)} %get-tuple-element.1176, f32[32,512]{1,0:T(8,128)S(1)} %get-tuple-element.1181, f32[64]{0:T(128)S(1)} %add_multiply_fusion.3, f32[32,64]{1,0:T(8,128)S(1)} %get-tuple-element.1182, ...), kind=kLoop, calls=%fused_computation.61.clone.1 | loop fusion | flops 15663104 | bytes 491776 | tf_op jit(solution)/shard_map/while/body/eval_jaxpr/reduce_sum | solution.py:200
  574.6 16.8 %fusion.295 = (f32[64,512]{1,0:T(8,128)S(1)}, f32[64,512]{1,0:T(8,128)S(1)}) fusion(f32[32,64]{1,0:T(8,128)S(1)} %get-tuple-element.1175, f32[32,64]{1,0:T(8,128)S(1)} %get-tuple-element.1176, f32[32,512]{1,0:T(8,128)S(1)} %get-tuple-element.1181, f32[64]{0:T(128)S(1)} %add_multiply_fusion.3, f32[32,64]{1,0:T(8,128)S(1)} %get-tuple-element.1182, ...), kind=kLoop, calls=%fused_computation.61.clone.1 | loop fusion | flops 15663104 | bytes 491776 | tf_op jit(solution)/shard_map/while/body/eval_jaxpr/reduce_sum | solution.py:200
  592.4 74.4 %reduce-scatter.2.cloned.1.call-done = f32[32,128]{1,0:T(8,128)} async-done(((f32[512,128]{1,0:T(8,128)}), f32[32,128]{1,0:T(8,128)}) %reduce-scatter.2.cloned.1.call-update) | async-done | bytes 16400 | tf_op jit(solution)/shard_map/reduce_scatter | solution.py:331
  (1784 shorter events, 331.1 us)
Async XLA Ops:
  11.5 11.5 %copy-start.426 = (bf16[3,64]{1,0:T(4,128)(2,1)S(1)}, bf16[3,64]{1,0:T(4,128)(2,1)}, u32[]{:S(2)}) copy-start(bf16[3,64]{1,0:T(4,128)(2,1)} %param.148) | copy-start | bytes 1156
  12.2 19.8 %collective-permute-start = (f32[10,1,1024]{2,1,0:T(1,128)S(1)}, f32[10,1,1024]{2,1,0:T(1,128)S(1)}, u32[]{:S(2)}, u32[]{:S(2)}) collective-permute-start(f32[10,1,1024]{2,1,0:T(1,128)S(1)} %get-tuple-element.752), channel_id=1, source_target_pairs={{0,1},{1,0},{2,3},{3,2},{4,5},{5,4},{6,7},{7,6},{8,9},{9,8},{10,11... | collective-permute-start | bytes 122888 | tf_op jit(solution)/shard_map/ppermute | solution.py:50
  12.7 18.4 %collective-permute-start.1 = (f32[10,1,1024]{2,1,0:T(1,128)S(1)}, f32[10,1,1024]{2,1,0:T(1,128)S(1)}, u32[]{:S(2)}, u32[]{:S(2)}) collective-permute-start(f32[10,1,1024]{2,1,0:T(1,128)S(1)} %get-tuple-element.753), channel_id=1, source_target_pairs={{1,0},{0,1},{3,2},{2,3},{5,4},{4,5},{7,6},{6,7},{9,8},{8,9},{11,10... | collective-permute-start | bytes 122888 | tf_op jit(solution)/shard_map/ppermute | solution.py:53
  16.8 14.2 %copy-start.420 = (s32[1024]{0:T(1024)}, s32[1024]{0:T(1024)S(1)}, u32[]{:S(2)}) copy-start(s32[1024]{0:T(1024)S(1)} %get-tuple-element.1095) | copy-start | bytes 12292
  77.0 12.0 %copy-start.161 = (f32[16,992]{1,0:T(8,128)S(1)}, f32[16,992]{1,0:T(8,128)}, u32[]{:S(2)}) copy-start(f32[16,992]{1,0:T(8,128)} %get-tuple-element.1039) | copy-start | bytes 190468
  77.0 12.0 %copy-start.320 = (f32[16,32]{1,0:T(8,128)S(1)}, f32[16,32]{1,0:T(8,128)}, u32[]{:S(2)}) copy-start(f32[16,32]{1,0:T(8,128)} %get-tuple-element.1037) | copy-start | bytes 6148
  77.0 12.1 %copy-start.164 = (f32[16,992]{1,0:T(8,128)S(1)}, f32[16,992]{1,0:T(8,128)}, u32[]{:S(2)}) copy-start(f32[16,992]{1,0:T(8,128)} %get-tuple-element.1045) | copy-start | bytes 190468
  77.0 12.1 %copy-start.323 = (f32[16,32]{1,0:T(8,128)S(1)}, f32[16,32]{1,0:T(8,128)}, u32[]{:S(2)}) copy-start(f32[16,32]{1,0:T(8,128)} %get-tuple-element.1047) | copy-start | bytes 6148
  77.0 12.1 %copy-start.167 = (f32[16,1023]{1,0:T(8,128)S(1)}, f32[16,1023]{1,0:T(8,128)}, u32[]{:S(2)}) copy-start(f32[16,1023]{1,0:T(8,128)} %get-tuple-element.1055) | copy-start | bytes 196420
  77.0 12.1 %copy-start.326 = (f32[16,1]{1,0:T(8,128)S(1)}, f32[16,1]{1,0:T(8,128)}, u32[]{:S(2)}) copy-start(f32[16,1]{1,0:T(8,128)} %get-tuple-element.1053) | copy-start | bytes 196
  77.0 12.2 %copy-start.170 = (f32[16,992]{1,0:T(8,128)S(1)}, f32[16,992]{1,0:T(8,128)}, u32[]{:S(2)}) copy-start(f32[16,992]{1,0:T(8,128)} %get-tuple-element.1041) | copy-start | bytes 190468
  77.1 12.2 %copy-start.329 = (f32[16,32]{1,0:T(8,128)S(1)}, f32[16,32]{1,0:T(8,128)}, u32[]{:S(2)}) copy-start(f32[16,32]{1,0:T(8,128)} %get-tuple-element.1043) | copy-start | bytes 6148
  78.6 10.8 %copy-start.173 = (f32[16,992]{1,0:T(8,128)S(1)}, f32[16,992]{1,0:T(8,128)}, u32[]{:S(2)}) copy-start(f32[16,992]{1,0:T(8,128)} %get-tuple-element.1051) | copy-start | bytes 190468
  78.6 10.8 %copy-start.332 = (f32[16,32]{1,0:T(8,128)S(1)}, f32[16,32]{1,0:T(8,128)}, u32[]{:S(2)}) copy-start(f32[16,32]{1,0:T(8,128)} %get-tuple-element.1049) | copy-start | bytes 6148
  78.6 10.8 %copy-start.176 = (f32[16,1023]{1,0:T(8,128)S(1)}, f32[16,1023]{1,0:T(8,128)}, u32[]{:S(2)}) copy-start(f32[16,1023]{1,0:T(8,128)} %get-tuple-element.1057) | copy-start | bytes 196420
  78.6 10.8 %copy-start.335 = (f32[16,1]{1,0:T(8,128)S(1)}, f32[16,1]{1,0:T(8,128)}, u32[]{:S(2)}) copy-start(f32[16,1]{1,0:T(8,128)} %get-tuple-element.1059) | copy-start | bytes 196
  78.7 10.8 %copy-start.179 = (f32[16,1023]{1,0:T(8,128)S(1)}, f32[16,1023]{1,0:T(8,128)}, u32[]{:S(2)}) copy-start(f32[16,1023]{1,0:T(8,128)} %get-tuple-element.1067) | copy-start | bytes 196420
  78.7 10.8 %copy-start.338 = (f32[16,1]{1,0:T(8,128)S(1)}, f32[16,1]{1,0:T(8,128)}, u32[]{:S(2)}) copy-start(f32[16,1]{1,0:T(8,128)} %get-tuple-element.1065) | copy-start | bytes 196
  78.7 10.9 %copy-start.184 = (f32[16,1023]{1,0:T(8,128)S(1)}, f32[16,1023]{1,0:T(8,128)}, u32[]{:S(2)}) copy-start(f32[16,1023]{1,0:T(8,128)} %get-tuple-element.1061) | copy-start | bytes 196420
  78.8 10.9 %copy-start.341 = (f32[16,1]{1,0:T(8,128)S(1)}, f32[16,1]{1,0:T(8,128)}, u32[]{:S(2)}) copy-start(f32[16,1]{1,0:T(8,128)} %get-tuple-element.1063) | copy-start | bytes 196
  78.9 10.8 %copy-start.191 = (f32[16,992]{1,0:T(8,128)S(1)}, f32[16,992]{1,0:T(8,128)}, u32[]{:S(2)}) copy-start(f32[16,992]{1,0:T(8,128)} %get-tuple-element.1023) | copy-start | bytes 190468
  78.9 10.8 %copy-start.347 = (f32[16,32]{1,0:T(8,128)S(1)}, f32[16,32]{1,0:T(8,128)}, u32[]{:S(2)}) copy-start(f32[16,32]{1,0:T(8,128)} %get-tuple-element.1021) | copy-start | bytes 6148
  79.1 10.7 %copy-start.194 = (f32[16,992]{1,0:T(8,128)S(1)}, f32[16,992]{1,0:T(8,128)}, u32[]{:S(2)}) copy-start(f32[16,992]{1,0:T(8,128)} %get-tuple-element.1025) | copy-start | bytes 190468
  79.1 10.7 %copy-start.350 = (f32[16,32]{1,0:T(8,128)S(1)}, f32[16,32]{1,0:T(8,128)}, u32[]{:S(2)}) copy-start(f32[16,32]{1,0:T(8,128)} %get-tuple-element.1027) | copy-start | bytes 6148
  79.3 10.6 %copy-start.197 = (f32[16,1023]{1,0:T(8,128)S(1)}, f32[16,1023]{1,0:T(8,128)}, u32[]{:S(2)}) copy-start(f32[16,1023]{1,0:T(8,128)} %get-tuple-element.1031) | copy-start | bytes 196420
  79.3 10.6 %copy-start.353 = (f32[16,1]{1,0:T(8,128)S(1)}, f32[16,1]{1,0:T(8,128)}, u32[]{:S(2)}) copy-start(f32[16,1]{1,0:T(8,128)} %get-tuple-element.1029) | copy-start | bytes 196
  79.3 10.7 %copy-start.200 = (f32[16,1023]{1,0:T(8,128)S(1)}, f32[16,1023]{1,0:T(8,128)}, u32[]{:S(2)}) copy-start(f32[16,1023]{1,0:T(8,128)} %get-tuple-element.1033) | copy-start | bytes 196420
  79.3 10.7 %copy-start.356 = (f32[16,1]{1,0:T(8,128)S(1)}, f32[16,1]{1,0:T(8,128)}, u32[]{:S(2)}) copy-start(f32[16,1]{1,0:T(8,128)} %get-tuple-element.1035) | copy-start | bytes 196
  79.7 10.5 %copy-start.206 = (f32[16,991]{1,0:T(8,128)S(1)}, f32[16,991]{1,0:T(8,128)}, u32[]{:S(2)}) copy-start(f32[16,991]{1,0:T(8,128)} %get-tuple-element.1073) | copy-start | bytes 190276
  79.7 10.5 %copy-start.362 = (f32[16,33]{1,0:T(8,128)S(1)}, f32[16,33]{1,0:T(8,128)}, u32[]{:S(2)}) copy-start(f32[16,33]{1,0:T(8,128)} %get-tuple-element.1075) | copy-start | bytes 6340
  80.6 20.7 %all-to-all-start = ((f32[16,1,2880]{2,1,0:T(1,128)}), f32[16,1,2880]{2,1,0:T(1,128)S(1)}, u32[]{:S(2)}, u32[]{:S(2)}) async-start(f32[16,1,2880]{2,1,0:T(1,128)} %copy.680), calls=%async_computation | async-start | bytes 376832 | tf_op jit(solution)/shard_map/all_to_all | solution.py:149
  90.3 10.9 %copy-start.2 = (f32[19,16,1024]{2,1,0:T(8,128)S(1)}, f32[19,16,1024]{2,1,0:T(8,128)}, u32[]{:S(2)}) copy-start(f32[19,16,1024]{2,1,0:T(8,128)} %get-tuple-element.745) | copy-start | bytes 3735556
  90.3 10.9 %copy-start.77 = (f32[1,16,1024]{2,1,0:T(8,128)S(1)}, f32[1,16,1024]{2,1,0:T(8,128)}, u32[]{:S(2)}) copy-start(f32[1,16,1024]{2,1,0:T(8,128)} %get-tuple-element.702) | copy-start | bytes 196612
  90.4 10.9 %copy-start.75 = (f32[1,16,1024]{2,1,0:T(8,128)S(1)}, f32[1,16,1024]{2,1,0:T(8,128)}, u32[]{:S(2)}) copy-start(f32[1,16,1024]{2,1,0:T(8,128)} %get-tuple-element.701) | copy-start | bytes 196612
  137.3 10.6 %copy-start.21 = (f32[1,16,1023]{2,1,0:T(8,128)S(1)}, f32[1,16,1023]{2,1,0:T(8,128)}, u32[]{:S(2)}) copy-start(f32[1,16,1023]{2,1,0:T(8,128)} %get-tuple-element.1068) | copy-start | bytes 196420
  154.7 5.0 collective-permute-start.2
  154.7 4.1 collective-permute-start.3
  209.7 19.7 %all-to-all-start.1 = ((f32[16,1,2880]{2,1,0:T(1,128)}), f32[16,1,2880]{2,1,0:T(1,128)S(1)}, u32[]{:S(2)}, u32[]{:S(2)}) async-start(f32[16,1,2880]{2,1,0:T(1,128)} %copy.703), calls=%async_computation.1 | async-start | bytes 376832 | tf_op jit(solution)/shard_map/all_to_all | solution.py:149
  218.2 10.4 %copy-start.187 = (f32[16,993]{1,0:T(8,128)S(1)}, f32[16,993]{1,0:T(8,128)}, u32[]{:S(2)}) copy-start(f32[16,993]{1,0:T(8,128)} %get-tuple-element.953) | copy-start | bytes 190660
  218.4 11.0 %copy-start.3 = (f32[19,16,1024]{2,1,0:T(8,128)S(1)}, f32[19,16,1024]{2,1,0:T(8,128)}, u32[]{:S(2)}) copy-start(f32[19,16,1024]{2,1,0:T(8,128)} %get-tuple-element.735) | copy-start | bytes 3735556
  218.4 11.0 %copy-start.81 = (f32[1,16,1024]{2,1,0:T(8,128)S(1)}, f32[1,16,1024]{2,1,0:T(8,128)}, u32[]{:S(2)}) copy-start(f32[1,16,1024]{2,1,0:T(8,128)} %get-tuple-element.692) | copy-start | bytes 196612
  218.5 10.9 %copy-start.79 = (f32[1,16,1024]{2,1,0:T(8,128)S(1)}, f32[1,16,1024]{2,1,0:T(8,128)}, u32[]{:S(2)}) copy-start(f32[1,16,1024]{2,1,0:T(8,128)} %get-tuple-element.691) | copy-start | bytes 196612
  265.6 10.6 %copy-start.22 = (f32[1,16,1023]{2,1,0:T(8,128)S(1)}, f32[1,16,1023]{2,1,0:T(8,128)}, u32[]{:S(2)}) copy-start(f32[1,16,1023]{2,1,0:T(8,128)} %get-tuple-element.940) | copy-start | bytes 196420
  282.9 4.9 collective-permute-start.4
  282.9 4.1 collective-permute-start.5
  337.9 19.5 %all-to-all-start.2 = ((f32[16,1,2880]{2,1,0:T(1,128)}), f32[16,1,2880]{2,1,0:T(1,128)S(1)}, u32[]{:S(2)}, u32[]{:S(2)}) async-start(f32[16,1,2880]{2,1,0:T(1,128)} %copy.726), calls=%async_computation.2 | async-start | bytes 376832 | tf_op jit(solution)/shard_map/all_to_all | solution.py:149
  346.4 11.0 %copy-start.4 = (f32[19,16,1024]{2,1,0:T(8,128)S(1)}, f32[19,16,1024]{2,1,0:T(8,128)}, u32[]{:S(2)}) copy-start(f32[19,16,1024]{2,1,0:T(8,128)} %get-tuple-element.725) | copy-start | bytes 3735556
  346.4 11.0 %copy-start.85 = (f32[1,16,1024]{2,1,0:T(8,128)S(1)}, f32[1,16,1024]{2,1,0:T(8,128)}, u32[]{:S(2)}) copy-start(f32[1,16,1024]{2,1,0:T(8,128)} %get-tuple-element.682) | copy-start | bytes 196612
  346.5 10.9 %copy-start.83 = (f32[1,16,1024]{2,1,0:T(8,128)S(1)}, f32[1,16,1024]{2,1,0:T(8,128)}, u32[]{:S(2)}) copy-start(f32[1,16,1024]{2,1,0:T(8,128)} %get-tuple-element.681) | copy-start | bytes 196612
  393.5 10.6 %copy-start.23 = (f32[1,16,1023]{2,1,0:T(8,128)S(1)}, f32[1,16,1023]{2,1,0:T(8,128)}, u32[]{:S(2)}) copy-start(f32[1,16,1023]{2,1,0:T(8,128)} %get-tuple-element.1004) | copy-start | bytes 196420
  410.9 5.0 collective-permute-start.6
  410.9 4.1 collective-permute-start.7
  451.6 10.6 %copy-start.183 = (f32[2,8,8,128]{3,2,1,0:T(8,128)S(1)}, f32[2,8,8,128]{3,2,1,0:T(8,128)}, u32[]{:S(2)}) copy-start(f32[2,8,8,128]{3,2,1,0:T(8,128)} %get-tuple-element.670) | copy-start | bytes 196612
  451.7 10.5 %copy-start.182 = (f32[1,16,1024]{2,1,0:T(8,128)S(1)}, f32[1,16,1024]{2,1,0:T(8,128)}, u32[]{:S(2)}) copy-start(f32[1,16,1024]{2,1,0:T(8,128)} %get-tuple-element.671) | copy-start | bytes 196612
  453.9 20.2 %copy-start.404 = (pred[8]{0:T(512)(128)(4,1)S(1)}, pred[8]{0:T(512)(128)(4,1)}, u32[]{:S(2)}) copy-start(pred[8]{0:T(512)(128)(4,1)} %get-tuple-element.651) | copy-start | bytes 28
  453.9 15.4 %all-to-all-start.3 = ((f32[16,1,2880]{2,1,0:T(1,128)}), f32[16,1,2880]{2,1,0:T(1,128)S(1)}, u32[]{:S(2)}, u32[]{:S(2)}) async-start(f32[16,1,2880]{2,1,0:T(1,128)} %copy.749), calls=%async_computation.3 | async-start | bytes 376832 | tf_op jit(solution)/shard_map/all_to_all | solution.py:149
  461.5 12.9 %copy-start.414 = (s32[5]{0:T(128)S(1)}, s32[5]{0:T(128)}, u32[]{:S(2)}) copy-start(s32[5]{0:T(128)} %constant.1290) | copy-start | bytes 64
  469.3 35.7 %all-to-all-start.5 = ((s32[16,1,8]{2,1,0:T(1,128)}), s32[16,1,8]{2,1,0:T(1,128)S(1)}, u32[]{:S(2)}, u32[]{:S(2)}) async-start(s32[16,1,8]{2,1,0:T(1,128)} %bitcast.352), calls=%async_computation.5 | async-start | bytes 16384 | tf_op jit(solution)/shard_map/all_to_all | solution.py:317
  502.8 17.4 %copy-start.370 = (bf16[256,64]{0,1:T(8,128)(2,1)S(1)}, bf16[256,64]{0,1:T(8,128)(2,1)}, u32[]{:S(2)}) copy-start(bf16[256,64]{0,1:T(8,128)(2,1)} %get-tuple-element.1085) | copy-start | bytes 98308
  502.8 17.3 %copy-start.371 = (bf16[256,64]{0,1:T(8,128)(2,1)S(1)}, bf16[256,64]{0,1:T(8,128)(2,1)}, u32[]{:S(2)}) copy-start(bf16[256,64]{0,1:T(8,128)(2,1)} %get-tuple-element.1086) | copy-start | bytes 98308
  503.2 19.2 %copy-start.265 = (f32[3,512]{1,0:T(4,128)S(1)}, f32[3,512]{1,0:T(4,128)}, u32[]{:S(2)}) copy-start(f32[3,512]{1,0:T(4,128)} %param.149) | copy-start | bytes 18436
  503.2 19.2 %copy-start.307 = (bf16[128,3]{0,1:T(4,128)(2,1)S(1)}, bf16[128,3]{0,1:T(4,128)(2,1)}, u32[]{:S(2)}) copy-start(bf16[128,3]{0,1:T(4,128)(2,1)} %reshape.9282) | copy-start | bytes 2308
  505.0 14.8 %all-to-all-start.4 = ((bf16[16,8,512]{2,1,0:T(8,128)(2,1)}), bf16[16,8,512]{2,1,0:T(8,128)(2,1)S(1)}, u32[]{:S(2)}, u32[]{:S(2)}) async-start(bf16[16,8,512]{2,1,0:T(8,128)(2,1)} %bitcast_select_fusion), calls=%async_computation.4 | async-start | bytes 262144 | tf_op jit(solution)/shard_map/all_to_all | solution.py:316
  512.0 154.8 %reduce-scatter.2.cloned.1.call-start = ((), (), s32[]{:S(2)}) async-start(), calls=%async_computation.7 | async-start | bytes 278528 | tf_op jit(solution)/shard_map/reduce_scatter | solution.py:331
  (383 other events, 2101.7 us)
Sparse Core Ops, SparseCore 0:
  592.5 74.2 reduce-scatter.1
where the time goes:
time: 686 us; the launch traced here: 674 us
  local copies, waits for them, and re-layouts  360 us (52%)
  other arithmetic  153 us (22%)
  waiting for transfers between devices  87.7 us (13%)
  starting transfers between devices  43.1 us (6%)
  between operations  22.8 us (3%)
    reduce_scatter x1, waiting for transfers between devices, body(): lax.psum_scatter(partial_value, 'blk', scatter_dimension=0, tiled=True)  74.4 us
    reduce_sum x4, other arithmetic, radiate(): real_part = jnp.sum(weight_real * cosine + weight_imag * sine_part, axis=0)  67.3 us
    slice x96, local copies, waits for them, and re-layouts, stream_merged(): jnp.roll(widened[number, begin:begin + slab_depth], shift_y * BS + shift_...  63.9 us
    unnamed x110, other arithmetic  53.2 us
    concatenate x8, local copies, waits for them, and re-layouts, body(): widened = jnp.concatenate([lower_plane, collided, upper_plane], axis=1)  50.4 us
    another operation x120, local copies, waits for them, and re-layouts, stream_merged(): jnp.tile(row_values, (1, BS))  48.2 us
    reshape x80, local copies, waits for them, and re-layouts, stream_merged(): jnp.repeat(column_values, BS, axis=-1)  47.6 us
    unnamed x979, local copies, waits for them, and re-layouts  44.4 us
  transfers between devices with their start and end apart: 15, of which 3 were waited for; matrix products, arithmetic and copies ran while one was open for 14% of the time, Pallas kernels for 0%

commit v1 on v0

--- a/solution.py
+++ b/solution.py
@@ -41,6 +41,18 @@
 sound_speed = 0.5
 
 
+def in_blocks(shard, dim, size):
+    lengths = shard.shape
+    pieces = shard.reshape(*lengths[:dim], size, lengths[dim] // size, *lengths[dim + 1 :])
+    return jnp.moveaxis(pieces, dim, 0)
+
+
+def joined_along(pieces, dim):
+    pieces = jnp.moveaxis(pieces, 0, dim)
+    lengths = pieces.shape
+    return pieces.reshape(*lengths[:dim], lengths[dim] * lengths[dim + 1], *lengths[dim + 2 :])
+
+
 def padded(block, sides, width):
     for axis, dim in sides:
         count = lax.axis_size(axis)
@@ -146,9 +158,15 @@
         ]
     ).reshape(8, -1)
     targets = jnp.concatenate([block_faces, block_edges])
-    received = lax.all_to_all(
-        place_pieces(outgoing, targets, blocks), "blk", split_axis=0, concat_axis=0, tiled=True
-    )
+    shard = place_pieces(outgoing, targets, blocks)
+    size, mine = (lax.axis_size("blk"), lax.axis_index("blk"))
+    shards = in_blocks(shard, 0, size)
+    done = [shards[mine]]
+    for step in range(1, size):
+        sent = shards[(mine + step) % size]
+        done.append(lax.ppermute(sent, "blk", [(i_2, (i_2 + step) % size) for i_2 in range(size)]))
+    shards = jnp.stack(done)[(mine - jnp.arange(size)) % size]
+    received = joined_along(shards, 0)
     chosen = jnp.take(received, targets, axis=0).reshape(8, 5, depth_x, BS)
     below_plane = spread_pops(chosen[0], y_upward, (19, depth_x, BS))
     above_plane = spread_pops(chosen[1], y_downward, (19, depth_x, BS))

time: 686 us -> 816 us (1.19)
  starting transfers between devices: 43.1 us -> 125 us
  other arithmetic: 153 us -> 179 us
  local copies, waits for them, and re-layouts: 360 us -> 380 us
    ppermute x0 -> x60, starting transfers between devices: none -> 111 us  [direct_halo(): lax.ppermute(sent, 'blk', [(i_2, (i_2 + step) % size) for i_2 in range(si...]
    all_to_all x4 -> x0, starting transfers between devices: 29.8 us -> none  [direct_halo(): lax.all_to_all(place_pieces(outgoing, targets, blocks), 'blk', split_axis...]
    unnamed x110, other arithmetic: 53.2 us -> 77.5 us
    another operation x20 -> x24, local copies, waits for them, and re-layouts: 0.3 us -> 8.49 us  [the longest x4 5.91 us: direct_halo(): shards = jnp.stack(done)[(mine - jnp.arange(size)) % size]]
    unnamed x979 -> x947, local copies, waits for them, and re-layouts: 44.4 us -> 46.3 us
  transfers between devices with their start and end apart: 15 -> 71, of which waited for: 3 -> 5; matrix products, arithmetic and copies ran while one was open for 14% -> 60% of each run, Pallas kernels for 0% -> 0%
where the time goes in v1:
time: 816 us; the launch traced here: 802 us
  local copies, waits for them, and re-layouts  380 us (47%)
  other arithmetic  179 us (22%)
  starting transfers between devices  125 us (15%)
  waiting for transfers between devices  87.2 us (11%)
  between operations  22.8 us (3%)
    ppermute x60, starting transfers between devices, direct_halo(): lax.ppermute(sent, 'blk', [(i_2, (i_2 + step) % size) for i_2 in range(si...  111 us
    unnamed x110, other arithmetic  77.5 us
    reduce_scatter x1, waiting for transfers between devices, body(): lax.psum_scatter(partial_value, 'blk', scatter_dimension=0, tiled=True)  74.4 us
    reduce_sum x4, other arithmetic, radiate(): real_part = jnp.sum(weight_real * cosine + weight_imag * sine_part, axis=0)  67.3 us
    slice x96, local copies, waits for them, and re-layouts, stream_merged(): jnp.roll(widened[number, begin:begin + slab_depth], shift_y * BS + shift_...  64 us
    concatenate x8, local copies, waits for them, and re-layouts, body(): widened = jnp.concatenate([lower_plane, collided, upper_plane], axis=1)  50.6 us
    another operation x120, local copies, waits for them, and re-layouts, stream_merged(): jnp.tile(row_values, (1, BS))  48.1 us
    reshape x80, local copies, waits for them, and re-layouts, stream_merged(): jnp.repeat(column_values, BS, axis=-1)  47.6 us
  transfers between devices with their start and end apart: 71, of which 5 were waited for; matrix products, arithmetic and copies ran while one was open for 60% of the time, Pallas kernels for 0%

profile of v1, /device:TPU:0, one launch (start us, length us, event | category | flops | bytes accessed | tf_op | source)
XLA Modules:
  0.0 802.2 jit_solution(17869407739319661460)
XLA Ops:
  10.1 1.6 gather_fusion.25
  12.4 8.4 %all-to-all-start.1 = ((s32[16,1,8]{2,1,0:T(1,128)}), s32[16,1,8]{2,1,0:T(1,128)}, u32[]{:S(2)}, u32[]{:S(2)}) async-start(s32[16,1,8]{2,1,0:T(1,128)} %bitcast.417), calls=%async_computation.1 | async-start | bytes 16384 | tf_op jit(solution)/shard_map/all_to_all | solution.py:335
  31.4 1.8 all-gather.1
  33.3 1.8 all-gather
  66.6 5.2 copy.660
  71.8 7.4 copy.656
  80.1 2.7 gather_fusion.4
  82.8 2.7 gather_fusion.3
  91.8 5.5 collective-permute-start.16
  99.0 1.7 collective-permute-start.12
  110.0 4.1 collective-permute-start.11
  115.7 2.9 collective-permute-start.8
  118.6 2.4 collective-permute-start.7
  121.6 1.8 collective-permute-start.5
  123.5 3.3 collective-permute-start.4
  139.5 1.9 stack.463
  226.7 5.2 copy.682
  231.9 3.3 gather_fusion.10
  235.2 3.3 gather_fusion.9
  238.5 7.4 copy.678
  254.4 5.7 collective-permute-start.33
  261.0 2.1 collective-permute-start.30
  273.3 3.8 collective-permute-start.28
  278.7 3.7 collective-permute-start.25
  284.0 1.6 collective-permute-start.23
  286.4 3.3 collective-permute-start.21
  289.7 2.6 collective-permute-start.20
  304.2 1.9 stack.493
  364.1 1.8 gather_fusion.31
  391.2 5.2 copy.704
  396.4 3.3 gather_fusion.16
  399.7 3.3 gather_fusion.15
  403.0 7.4 copy.700
  418.9 5.7 collective-permute-start.50
  424.6 1.6 collective-permute-start.47
  436.6 4.1 collective-permute-start.45
  440.8 1.9 collective-permute-start.43
  442.7 2.8 collective-permute-start.42
  445.5 2.0 collective-permute-start.41
  450.1 3.3 collective-permute-start.38
  453.3 2.1 collective-permute-start.37
  467.1 1.9 stack.523
  527.0 1.8 gather_fusion.32
  543.9 5.2 copy.726
  549.1 2.7 gather_fusion.22
  551.8 2.7 gather_fusion.21
  554.4 7.5 copy.722
  567.4 5.7 collective-permute-start.67
  573.7 2.1 collective-permute-start.64
  577.2 3.8 collective-permute-start.62
  582.6 3.8 collective-permute-start.59
  590.4 3.4 collective-permute-start.55
  593.8 2.9 collective-permute-start.54
  598.3 1.8 collective-permute-done.54
  600.1 4.0 collective-permute-done.53
  636.9 3.5 all-to-all-start
  642.1 6.1 all-to-all-done
  648.7 2.1 all_gather.11
  650.8 69.2 %while.46 = (s32[]{:T(128)}, f32[512,128]{0,1:T(8,128)S(1)}, bf16[3,128]{1,0:T(4,128)(2,1)S(1)}, f32[3,512]{1,0:T(4,128)S(1)}, bf16[3,128]{1,0:T(4,128)(2,1)S(1)...) while((s32[]{:T(128)}, f32[512,128]{0,1:T(8,128)S(1)}, ...), condition=%wide.region_46.49_spmd.clone, body=%wide.region_41.48_spmd.clone.sunk | while | flops 16179527 | bytes 1860141 | solution.py:241
  651.1 16.8 %fusion.305 = (f32[64,512]{1,0:T(8,128)S(1)}, f32[64,512]{1,0:T(8,128)S(1)}) fusion(f32[32,64]{1,0:T(8,128)S(1)} %get-tuple-element.1239, f32[32,64]{1,0:T(8,128)S(1)} %get-tuple-element.1240, f32[32,512]{1,0:T(8,128)S(1)} %get-tuple-element.1245, f32[64]{0:T(128)S(1)} %add_multiply_fusion.3, f32[32,64]{1,0:T(8,128)S(1)} %get-tuple-element.1246, ...), kind=kLoop, calls=%fused_computation.65.clone.1 | loop fusion | flops 15663104 | bytes 491776 | tf_op jit(solution)/shard_map/while/body/eval_jaxpr/reduce_sum | solution.py:218
  668.4 16.8 %fusion.305 = (f32[64,512]{1,0:T(8,128)S(1)}, f32[64,512]{1,0:T(8,128)S(1)}) fusion(f32[32,64]{1,0:T(8,128)S(1)} %get-tuple-element.1239, f32[32,64]{1,0:T(8,128)S(1)} %get-tuple-element.1240, f32[32,512]{1,0:T(8,128)S(1)} %get-tuple-element.1245, f32[64]{0:T(128)S(1)} %add_multiply_fusion.3, f32[32,64]{1,0:T(8,128)S(1)} %get-tuple-element.1246, ...), kind=kLoop, calls=%fused_computation.65.clone.1 | loop fusion | flops 15663104 | bytes 491776 | tf_op jit(solution)/shard_map/while/body/eval_jaxpr/reduce_sum | solution.py:218
  685.7 16.8 %fusion.305 = (f32[64,512]{1,0:T(8,128)S(1)}, f32[64,512]{1,0:T(8,128)S(1)}) fusion(f32[32,64]{1,0:T(8,128)S(1)} %get-tuple-element.1239, f32[32,64]{1,0:T(8,128)S(1)} %get-tuple-element.1240, f32[32,512]{1,0:T(8,128)S(1)} %get-tuple-element.1245, f32[64]{0:T(128)S(1)} %add_multiply_fusion.3, f32[32,64]{1,0:T(8,128)S(1)} %get-tuple-element.1246, ...), kind=kLoop, calls=%fused_computation.65.clone.1 | loop fusion | flops 15663104 | bytes 491776 | tf_op jit(solution)/shard_map/while/body/eval_jaxpr/reduce_sum | solution.py:218
  703.0 16.8 %fusion.305 = (f32[64,512]{1,0:T(8,128)S(1)}, f32[64,512]{1,0:T(8,128)S(1)}) fusion(f32[32,64]{1,0:T(8,128)S(1)} %get-tuple-element.1239, f32[32,64]{1,0:T(8,128)S(1)} %get-tuple-element.1240, f32[32,512]{1,0:T(8,128)S(1)} %get-tuple-element.1245, f32[64]{0:T(128)S(1)} %add_multiply_fusion.3, f32[32,64]{1,0:T(8,128)S(1)} %get-tuple-element.1246, ...), kind=kLoop, calls=%fused_computation.65.clone.1 | loop fusion | flops 15663104 | bytes 491776 | tf_op jit(solution)/shard_map/while/body/eval_jaxpr/reduce_sum | solution.py:218
  720.8 74.4 %reduce-scatter.2.cloned.1.call-done = f32[32,128]{1,0:T(8,128)} async-done(((f32[512,128]{1,0:T(8,128)}), f32[32,128]{1,0:T(8,128)}) %reduce-scatter.2.cloned.1.call-update) | async-done | bytes 16400 | tf_op jit(solution)/shard_map/reduce_scatter | solution.py:349
  (1874 shorter events, 433.2 us)
Async XLA Ops:
  12.4 624.5 %all-to-all-start.1 = ((s32[16,1,8]{2,1,0:T(1,128)}), s32[16,1,8]{2,1,0:T(1,128)}, u32[]{:S(2)}, u32[]{:S(2)}) async-start(s32[16,1,8]{2,1,0:T(1,128)} %bitcast.417), calls=%async_computation.1 | async-start | bytes 16384 | tf_op jit(solution)/shard_map/all_to_all | solution.py:335
  25.6 16.7 %collective-permute-start = (f32[10,1,1024]{2,1,0:T(1,128)S(1)}, f32[10,1,1024]{2,1,0:T(1,128)S(1)}, u32[]{:S(2)}, u32[]{:S(2)}) collective-permute-start(f32[10,1,1024]{2,1,0:T(1,128)S(1)} %get-tuple-element.752), channel_id=1, source_target_pairs={{0,1},{1,0},{2,3},{3,2},{4,5},{5,4},{6,7},{7,6},{8,9},{9,8},{10,11... | collective-permute-start | bytes 122888 | tf_op jit(solution)/shard_map/ppermute | solution.py:62
  25.7 15.7 %collective-permute-start.1 = (f32[10,1,1024]{2,1,0:T(1,128)S(1)}, f32[10,1,1024]{2,1,0:T(1,128)S(1)}, u32[]{:S(2)}, u32[]{:S(2)}) collective-permute-start(f32[10,1,1024]{2,1,0:T(1,128)S(1)} %get-tuple-element.753), channel_id=1, source_target_pairs={{1,0},{0,1},{3,2},{2,3},{5,4},{4,5},{7,6},{6,7},{9,8},{8,9},{11,10... | collective-permute-start | bytes 122888 | tf_op jit(solution)/shard_map/ppermute | solution.py:65
  91.8 18.2 %collective-permute-start.16 = (f32[1,2880]{1,0:T(1,128)S(1)}, f32[1,2880]{1,0:T(1,128)S(1)}, u32[]{:S(2)}, u32[]{:S(2)}) collective-permute-start(f32[1,2880]{1,0:T(1,128)S(1)} %get-tuple-element.898), channel_id=1, source_target_pairs={{0,30},{2,0},{4,2},{6,4},{8,6},{10,8},{12,10},{14,12},{16,14},{18,... | collective-permute-start | bytes 34568 | tf_op jit(solution)/shard_map/ppermute | solution.py:167
  97.4 16.7 %collective-permute-start.15 = (f32[1,2880]{1,0:T(1,128)S(1)}, f32[1,2880]{1,0:T(1,128)S(1)}, u32[]{:S(2)}, u32[]{:S(2)}) collective-permute-start(f32[1,2880]{1,0:T(1,128)S(1)} %get-tuple-element.899), channel_id=1, source_target_pairs={{0,28},{2,30},{4,0},{6,2},{8,4},{10,6},{12,8},{14,10},{16,12},{18,... | collective-permute-start | bytes 34568 | tf_op jit(solution)/shard_map/ppermute | solution.py:167
  97.9 16.3 %collective-permute-start.14 = (f32[1,2880]{1,0:T(1,128)S(1)}, f32[1,2880]{1,0:T(1,128)S(1)}, u32[]{:S(2)}, u32[]{:S(2)}) collective-permute-start(f32[1,2880]{1,0:T(1,128)S(1)} %get-tuple-element.900), channel_id=1, source_target_pairs={{0,26},{2,28},{4,30},{6,0},{8,2},{10,4},{12,6},{14,8},{16,10},{18,... | collective-permute-start | bytes 34568 | tf_op jit(solution)/shard_map/ppermute | solution.py:167
  98.4 17.2 %collective-permute-start.13 = (f32[1,2880]{1,0:T(1,128)S(1)}, f32[1,2880]{1,0:T(1,128)S(1)}, u32[]{:S(2)}, u32[]{:S(2)}) collective-permute-start(f32[1,2880]{1,0:T(1,128)S(1)} %get-tuple-element.901), channel_id=1, source_target_pairs={{0,24},{2,26},{4,28},{6,30},{8,0},{10,2},{12,4},{14,6},{16,8},{18,... | collective-permute-start | bytes 34568 | tf_op jit(solution)/shard_map/ppermute | solution.py:167
  99.0 19.5 %collective-permute-start.12 = (f32[1,2880]{1,0:T(1,128)S(1)}, f32[1,2880]{1,0:T(1,128)S(1)}, u32[]{:S(2)}, u32[]{:S(2)}) collective-permute-start(f32[1,2880]{1,0:T(1,128)S(1)} %get-tuple-element.902), channel_id=1, source_target_pairs={{0,22},{2,24},{4,26},{6,28},{8,30},{10,0},{12,2},{14,4},{16,6},{18... | collective-permute-start | bytes 34568 | tf_op jit(solution)/shard_map/ppermute | solution.py:167
  110.0 11.0 %collective-permute-start.11 = (f32[1,2880]{1,0:T(1,128)S(1)}, f32[1,2880]{1,0:T(1,128)S(1)}, u32[]{:S(2)}, u32[]{:S(2)}) collective-permute-start(f32[1,2880]{1,0:T(1,128)S(1)} %get-tuple-element.903), channel_id=1, source_target_pairs={{0,20},{2,22},{4,24},{6,26},{8,28},{10,30},{12,0},{14,2},{16,4},{1... | collective-permute-start | bytes 34568 | tf_op jit(solution)/shard_map/ppermute | solution.py:167
  114.1 7.5 collective-permute-start.10
  114.1 9.3 %collective-permute-start.9 = (f32[1,2880]{1,0:T(1,128)S(1)}, f32[1,2880]{1,0:T(1,128)S(1)}, u32[]{:S(2)}, u32[]{:S(2)}) collective-permute-start(f32[1,2880]{1,0:T(1,128)S(1)} %get-tuple-element.905), channel_id=1, source_target_pairs={{0,16},{2,18},{4,20},{6,22},{8,24},{10,26},{12,28},{14,30},{16,0},... | collective-permute-start | bytes 34568 | tf_op jit(solution)/shard_map/ppermute | solution.py:167
  115.7 11.1 %collective-permute-start.8 = (f32[1,2880]{1,0:T(1,128)S(1)}, f32[1,2880]{1,0:T(1,128)S(1)}, u32[]{:S(2)}, u32[]{:S(2)}) collective-permute-start(f32[1,2880]{1,0:T(1,128)S(1)} %get-tuple-element.906), channel_id=1, source_target_pairs={{0,14},{2,16},{4,18},{6,20},{8,22},{10,24},{12,26},{14,28},{16,30}... | collective-permute-start | bytes 34568 | tf_op jit(solution)/shard_map/ppermute | solution.py:167
  118.6 9.4 %collective-permute-start.7 = (f32[1,2880]{1,0:T(1,128)S(1)}, f32[1,2880]{1,0:T(1,128)S(1)}, u32[]{:S(2)}, u32[]{:S(2)}) collective-permute-start(f32[1,2880]{1,0:T(1,128)S(1)} %get-tuple-element.907), channel_id=1, source_target_pairs={{0,12},{2,14},{4,16},{6,18},{8,20},{10,22},{12,24},{14,26},{16,28}... | collective-permute-start | bytes 34568 | tf_op jit(solution)/shard_map/ppermute | solution.py:167
  121.1 17.8 %collective-permute-start.6 = (f32[1,2880]{1,0:T(1,128)S(1)}, f32[1,2880]{1,0:T(1,128)S(1)}, u32[]{:S(2)}, u32[]{:S(2)}) collective-permute-start(f32[1,2880]{1,0:T(1,128)S(1)} %get-tuple-element.908), channel_id=1, source_target_pairs={{0,10},{2,12},{4,14},{6,16},{8,18},{10,20},{12,22},{14,24},{16,26}... | collective-permute-start | bytes 34568 | tf_op jit(solution)/shard_map/ppermute | solution.py:167
  121.6 17.2 %collective-permute-start.5 = (f32[1,2880]{1,0:T(1,128)S(1)}, f32[1,2880]{1,0:T(1,128)S(1)}, u32[]{:S(2)}, u32[]{:S(2)}) collective-permute-start(f32[1,2880]{1,0:T(1,128)S(1)} %get-tuple-element.909), channel_id=1, source_target_pairs={{0,8},{2,10},{4,12},{6,14},{8,16},{10,18},{12,20},{14,22},{16,24},... | collective-permute-start | bytes 34568 | tf_op jit(solution)/shard_map/ppermute | solution.py:167
  123.5 15.4 %collective-permute-start.4 = (f32[1,2880]{1,0:T(1,128)S(1)}, f32[1,2880]{1,0:T(1,128)S(1)}, u32[]{:S(2)}, u32[]{:S(2)}) collective-permute-start(f32[1,2880]{1,0:T(1,128)S(1)} %get-tuple-element.910), channel_id=1, source_target_pairs={{0,6},{2,8},{4,10},{6,12},{8,14},{10,16},{12,18},{14,20},{16,22},{... | collective-permute-start | bytes 34568 | tf_op jit(solution)/shard_map/ppermute | solution.py:167
  126.8 12.1 %collective-permute-start.3 = (f32[1,2880]{1,0:T(1,128)S(1)}, f32[1,2880]{1,0:T(1,128)S(1)}, u32[]{:S(2)}, u32[]{:S(2)}) collective-permute-start(f32[1,2880]{1,0:T(1,128)S(1)} %get-tuple-element.911), channel_id=1, source_target_pairs={{0,4},{2,6},{4,8},{6,10},{8,12},{10,14},{12,16},{14,18},{16,20},{1... | collective-permute-start | bytes 34568 | tf_op jit(solution)/shard_map/ppermute | solution.py:167
  127.9 11.0 %collective-permute-start.2 = (f32[1,2880]{1,0:T(1,128)S(1)}, f32[1,2880]{1,0:T(1,128)S(1)}, u32[]{:S(2)}, u32[]{:S(2)}) collective-permute-start(f32[1,2880]{1,0:T(1,128)S(1)} %get-tuple-element.912), channel_id=1, source_target_pairs={{0,2},{2,4},{4,6},{6,8},{8,10},{10,12},{12,14},{14,16},{16,18},{18... | collective-permute-start | bytes 34568 | tf_op jit(solution)/shard_map/ppermute | solution.py:167
  254.4 18.9 %collective-permute-start.33 = (f32[1,2880]{1,0:T(1,128)S(1)}, f32[1,2880]{1,0:T(1,128)S(1)}, u32[]{:S(2)}, u32[]{:S(2)}) collective-permute-start(f32[1,2880]{1,0:T(1,128)S(1)} %get-tuple-element.882), channel_id=1, source_target_pairs={{0,30},{2,0},{4,2},{6,4},{8,6},{10,8},{12,10},{14,12},{16,14},{18,... | collective-permute-start | bytes 34568 | tf_op jit(solution)/shard_map/ppermute | solution.py:167
  260.1 17.0 %collective-permute-start.32 = (f32[1,2880]{1,0:T(1,128)S(1)}, f32[1,2880]{1,0:T(1,128)S(1)}, u32[]{:S(2)}, u32[]{:S(2)}) collective-permute-start(f32[1,2880]{1,0:T(1,128)S(1)} %get-tuple-element.883), channel_id=1, source_target_pairs={{0,28},{2,30},{4,0},{6,2},{8,4},{10,6},{12,8},{14,10},{16,12},{18,... | collective-permute-start | bytes 34568 | tf_op jit(solution)/shard_map/ppermute | solution.py:167
  260.9 16.7 %collective-permute-start.31 = (f32[1,2880]{1,0:T(1,128)S(1)}, f32[1,2880]{1,0:T(1,128)S(1)}, u32[]{:S(2)}, u32[]{:S(2)}) collective-permute-start(f32[1,2880]{1,0:T(1,128)S(1)} %get-tuple-element.884), channel_id=1, source_target_pairs={{0,26},{2,28},{4,30},{6,0},{8,2},{10,4},{12,6},{14,8},{16,10},{18,... | collective-permute-start | bytes 34568 | tf_op jit(solution)/shard_map/ppermute | solution.py:167
  261.0 17.6 %collective-permute-start.30 = (f32[1,2880]{1,0:T(1,128)S(1)}, f32[1,2880]{1,0:T(1,128)S(1)}, u32[]{:S(2)}, u32[]{:S(2)}) collective-permute-start(f32[1,2880]{1,0:T(1,128)S(1)} %get-tuple-element.885), channel_id=1, source_target_pairs={{0,24},{2,26},{4,28},{6,30},{8,0},{10,2},{12,4},{14,6},{16,8},{18,... | collective-permute-start | bytes 34568 | tf_op jit(solution)/shard_map/ppermute | solution.py:167
  263.1 19.3 %collective-permute-start.29 = (f32[1,2880]{1,0:T(1,128)S(1)}, f32[1,2880]{1,0:T(1,128)S(1)}, u32[]{:S(2)}, u32[]{:S(2)}) collective-permute-start(f32[1,2880]{1,0:T(1,128)S(1)} %get-tuple-element.886), channel_id=1, source_target_pairs={{0,22},{2,24},{4,26},{6,28},{8,30},{10,0},{12,2},{14,4},{16,6},{18... | collective-permute-start | bytes 34568 | tf_op jit(solution)/shard_map/ppermute | solution.py:167
  273.3 10.7 %collective-permute-start.28 = (f32[1,2880]{1,0:T(1,128)S(1)}, f32[1,2880]{1,0:T(1,128)S(1)}, u32[]{:S(2)}, u32[]{:S(2)}) collective-permute-start(f32[1,2880]{1,0:T(1,128)S(1)} %get-tuple-element.887), channel_id=1, source_target_pairs={{0,20},{2,22},{4,24},{6,26},{8,28},{10,30},{12,0},{14,2},{16,4},{1... | collective-permute-start | bytes 34568 | tf_op jit(solution)/shard_map/ppermute | solution.py:167
  277.1 8.5 %collective-permute-start.27 = (f32[1,2880]{1,0:T(1,128)S(1)}, f32[1,2880]{1,0:T(1,128)S(1)}, u32[]{:S(2)}, u32[]{:S(2)}) collective-permute-start(f32[1,2880]{1,0:T(1,128)S(1)} %get-tuple-element.888), channel_id=1, source_target_pairs={{0,18},{2,20},{4,22},{6,24},{8,26},{10,28},{12,30},{14,0},{16,2},{... | collective-permute-start | bytes 34568 | tf_op jit(solution)/shard_map/ppermute | solution.py:167
  277.7 8.7 %collective-permute-start.26 = (f32[1,2880]{1,0:T(1,128)S(1)}, f32[1,2880]{1,0:T(1,128)S(1)}, u32[]{:S(2)}, u32[]{:S(2)}) collective-permute-start(f32[1,2880]{1,0:T(1,128)S(1)} %get-tuple-element.889), channel_id=1, source_target_pairs={{0,16},{2,18},{4,20},{6,22},{8,24},{10,26},{12,28},{14,30},{16,0},... | collective-permute-start | bytes 34568 | tf_op jit(solution)/shard_map/ppermute | solution.py:167
  278.7 11.0 %collective-permute-start.25 = (f32[1,2880]{1,0:T(1,128)S(1)}, f32[1,2880]{1,0:T(1,128)S(1)}, u32[]{:S(2)}, u32[]{:S(2)}) collective-permute-start(f32[1,2880]{1,0:T(1,128)S(1)} %get-tuple-element.890), channel_id=1, source_target_pairs={{0,14},{2,16},{4,18},{6,20},{8,22},{10,24},{12,26},{14,28},{16,30}... | collective-permute-start | bytes 34568 | tf_op jit(solution)/shard_map/ppermute | solution.py:167
  282.4 9.8 %collective-permute-start.24 = (f32[1,2880]{1,0:T(1,128)S(1)}, f32[1,2880]{1,0:T(1,128)S(1)}, u32[]{:S(2)}, u32[]{:S(2)}) collective-permute-start(f32[1,2880]{1,0:T(1,128)S(1)} %get-tuple-element.891), channel_id=1, source_target_pairs={{0,12},{2,14},{4,16},{6,18},{8,20},{10,22},{12,24},{14,26},{16,28}... | collective-permute-start | bytes 34568 | tf_op jit(solution)/shard_map/ppermute | solution.py:167
  284.0 19.6 %collective-permute-start.23 = (f32[1,2880]{1,0:T(1,128)S(1)}, f32[1,2880]{1,0:T(1,128)S(1)}, u32[]{:S(2)}, u32[]{:S(2)}) collective-permute-start(f32[1,2880]{1,0:T(1,128)S(1)} %get-tuple-element.892), channel_id=1, source_target_pairs={{0,10},{2,12},{4,14},{6,16},{8,18},{10,20},{12,22},{14,24},{16,26}... | collective-permute-start | bytes 34568 | tf_op jit(solution)/shard_map/ppermute | solution.py:167
  285.6 18.0 %collective-permute-start.22 = (f32[1,2880]{1,0:T(1,128)S(1)}, f32[1,2880]{1,0:T(1,128)S(1)}, u32[]{:S(2)}, u32[]{:S(2)}) collective-permute-start(f32[1,2880]{1,0:T(1,128)S(1)} %get-tuple-element.893), channel_id=1, source_target_pairs={{0,8},{2,10},{4,12},{6,14},{8,16},{10,18},{12,20},{14,22},{16,24},... | collective-permute-start | bytes 34568 | tf_op jit(solution)/shard_map/ppermute | solution.py:167
  286.4 17.1 %collective-permute-start.21 = (f32[1,2880]{1,0:T(1,128)S(1)}, f32[1,2880]{1,0:T(1,128)S(1)}, u32[]{:S(2)}, u32[]{:S(2)}) collective-permute-start(f32[1,2880]{1,0:T(1,128)S(1)} %get-tuple-element.894), channel_id=1, source_target_pairs={{0,6},{2,8},{4,10},{6,12},{8,14},{10,16},{12,18},{14,20},{16,22},{... | collective-permute-start | bytes 34568 | tf_op jit(solution)/shard_map/ppermute | solution.py:167
  289.7 13.9 %collective-permute-start.20 = (f32[1,2880]{1,0:T(1,128)S(1)}, f32[1,2880]{1,0:T(1,128)S(1)}, u32[]{:S(2)}, u32[]{:S(2)}) collective-permute-start(f32[1,2880]{1,0:T(1,128)S(1)} %get-tuple-element.895), channel_id=1, source_target_pairs={{0,4},{2,6},{4,8},{6,10},{8,12},{10,14},{12,16},{14,18},{16,20},{1... | collective-permute-start | bytes 34568 | tf_op jit(solution)/shard_map/ppermute | solution.py:167
  292.3 11.3 %collective-permute-start.19 = (f32[1,2880]{1,0:T(1,128)S(1)}, f32[1,2880]{1,0:T(1,128)S(1)}, u32[]{:S(2)}, u32[]{:S(2)}) collective-permute-start(f32[1,2880]{1,0:T(1,128)S(1)} %get-tuple-element.896), channel_id=1, source_target_pairs={{0,2},{2,4},{4,6},{6,8},{8,10},{10,12},{12,14},{14,16},{16,18},{18... | collective-permute-start | bytes 34568 | tf_op jit(solution)/shard_map/ppermute | solution.py:167
  418.9 17.7 %collective-permute-start.50 = (f32[1,2880]{1,0:T(1,128)S(1)}, f32[1,2880]{1,0:T(1,128)S(1)}, u32[]{:S(2)}, u32[]{:S(2)}) collective-permute-start(f32[1,2880]{1,0:T(1,128)S(1)} %get-tuple-element.866), channel_id=1, source_target_pairs={{0,30},{2,0},{4,2},{6,4},{8,6},{10,8},{12,10},{14,12},{16,14},{18,... | collective-permute-start | bytes 34568 | tf_op jit(solution)/shard_map/ppermute | solution.py:167
  424.6 16.1 %collective-permute-start.49 = (f32[1,2880]{1,0:T(1,128)S(1)}, f32[1,2880]{1,0:T(1,128)S(1)}, u32[]{:S(2)}, u32[]{:S(2)}) collective-permute-start(f32[1,2880]{1,0:T(1,128)S(1)} %get-tuple-element.867), channel_id=1, source_target_pairs={{0,28},{2,30},{4,0},{6,2},{8,4},{10,6},{12,8},{14,10},{16,12},{18,... | collective-permute-start | bytes 34568 | tf_op jit(solution)/shard_map/ppermute | solution.py:167
  424.6 16.2 %collective-permute-start.48 = (f32[1,2880]{1,0:T(1,128)S(1)}, f32[1,2880]{1,0:T(1,128)S(1)}, u32[]{:S(2)}, u32[]{:S(2)}) collective-permute-start(f32[1,2880]{1,0:T(1,128)S(1)} %get-tuple-element.868), channel_id=1, source_target_pairs={{0,26},{2,28},{4,30},{6,0},{8,2},{10,4},{12,6},{14,8},{16,10},{18,... | collective-permute-start | bytes 34568 | tf_op jit(solution)/shard_map/ppermute | solution.py:167
  424.6 18.1 %collective-permute-start.47 = (f32[1,2880]{1,0:T(1,128)S(1)}, f32[1,2880]{1,0:T(1,128)S(1)}, u32[]{:S(2)}, u32[]{:S(2)}) collective-permute-start(f32[1,2880]{1,0:T(1,128)S(1)} %get-tuple-element.869), channel_id=1, source_target_pairs={{0,24},{2,26},{4,28},{6,30},{8,0},{10,2},{12,4},{14,6},{16,8},{18,... | collective-permute-start | bytes 34568 | tf_op jit(solution)/shard_map/ppermute | solution.py:167
  426.2 19.3 %collective-permute-start.46 = (f32[1,2880]{1,0:T(1,128)S(1)}, f32[1,2880]{1,0:T(1,128)S(1)}, u32[]{:S(2)}, u32[]{:S(2)}) collective-permute-start(f32[1,2880]{1,0:T(1,128)S(1)} %get-tuple-element.870), channel_id=1, source_target_pairs={{0,22},{2,24},{4,26},{6,28},{8,30},{10,0},{12,2},{14,4},{16,6},{18... | collective-permute-start | bytes 34568 | tf_op jit(solution)/shard_map/ppermute | solution.py:167
  436.6 11.0 %collective-permute-start.45 = (f32[1,2880]{1,0:T(1,128)S(1)}, f32[1,2880]{1,0:T(1,128)S(1)}, u32[]{:S(2)}, u32[]{:S(2)}) collective-permute-start(f32[1,2880]{1,0:T(1,128)S(1)} %get-tuple-element.871), channel_id=1, source_target_pairs={{0,20},{2,22},{4,24},{6,26},{8,28},{10,30},{12,0},{14,2},{16,4},{1... | collective-permute-start | bytes 34568 | tf_op jit(solution)/shard_map/ppermute | solution.py:167
  440.7 8.0 collective-permute-start.44
  440.8 9.2 %collective-permute-start.43 = (f32[1,2880]{1,0:T(1,128)S(1)}, f32[1,2880]{1,0:T(1,128)S(1)}, u32[]{:S(2)}, u32[]{:S(2)}) collective-permute-start(f32[1,2880]{1,0:T(1,128)S(1)} %get-tuple-element.873), channel_id=1, source_target_pairs={{0,16},{2,18},{4,20},{6,22},{8,24},{10,26},{12,28},{14,30},{16,0},... | collective-permute-start | bytes 34568 | tf_op jit(solution)/shard_map/ppermute | solution.py:167
  442.7 10.6 %collective-permute-start.42 = (f32[1,2880]{1,0:T(1,128)S(1)}, f32[1,2880]{1,0:T(1,128)S(1)}, u32[]{:S(2)}, u32[]{:S(2)}) collective-permute-start(f32[1,2880]{1,0:T(1,128)S(1)} %get-tuple-element.874), channel_id=1, source_target_pairs={{0,14},{2,16},{4,18},{6,20},{8,22},{10,24},{12,26},{14,28},{16,30}... | collective-permute-start | bytes 34568 | tf_op jit(solution)/shard_map/ppermute | solution.py:167
  445.5 9.8 %collective-permute-start.41 = (f32[1,2880]{1,0:T(1,128)S(1)}, f32[1,2880]{1,0:T(1,128)S(1)}, u32[]{:S(2)}, u32[]{:S(2)}) collective-permute-start(f32[1,2880]{1,0:T(1,128)S(1)} %get-tuple-element.875), channel_id=1, source_target_pairs={{0,12},{2,14},{4,16},{6,18},{8,20},{10,22},{12,24},{14,26},{16,28}... | collective-permute-start | bytes 34568 | tf_op jit(solution)/shard_map/ppermute | solution.py:167
  447.6 18.8 %collective-permute-start.40 = (f32[1,2880]{1,0:T(1,128)S(1)}, f32[1,2880]{1,0:T(1,128)S(1)}, u32[]{:S(2)}, u32[]{:S(2)}) collective-permute-start(f32[1,2880]{1,0:T(1,128)S(1)} %get-tuple-element.876), channel_id=1, source_target_pairs={{0,10},{2,12},{4,14},{6,16},{8,18},{10,20},{12,22},{14,24},{16,26}... | collective-permute-start | bytes 34568 | tf_op jit(solution)/shard_map/ppermute | solution.py:167
  448.7 17.8 %collective-permute-start.39 = (f32[1,2880]{1,0:T(1,128)S(1)}, f32[1,2880]{1,0:T(1,128)S(1)}, u32[]{:S(2)}, u32[]{:S(2)}) collective-permute-start(f32[1,2880]{1,0:T(1,128)S(1)} %get-tuple-element.877), channel_id=1, source_target_pairs={{0,8},{2,10},{4,12},{6,14},{8,16},{10,18},{12,20},{14,22},{16,24},... | collective-permute-start | bytes 34568 | tf_op jit(solution)/shard_map/ppermute | solution.py:167
  450.1 16.4 %collective-permute-start.38 = (f32[1,2880]{1,0:T(1,128)S(1)}, f32[1,2880]{1,0:T(1,128)S(1)}, u32[]{:S(2)}, u32[]{:S(2)}) collective-permute-start(f32[1,2880]{1,0:T(1,128)S(1)} %get-tuple-element.878), channel_id=1, source_target_pairs={{0,6},{2,8},{4,10},{6,12},{8,14},{10,16},{12,18},{14,20},{16,22},{... | collective-permute-start | bytes 34568 | tf_op jit(solution)/shard_map/ppermute | solution.py:167
  453.3 13.2 %collective-permute-start.37 = (f32[1,2880]{1,0:T(1,128)S(1)}, f32[1,2880]{1,0:T(1,128)S(1)}, u32[]{:S(2)}, u32[]{:S(2)}) collective-permute-start(f32[1,2880]{1,0:T(1,128)S(1)} %get-tuple-element.879), channel_id=1, source_target_pairs={{0,4},{2,6},{4,8},{6,10},{8,12},{10,14},{12,16},{14,18},{16,20},{1... | collective-permute-start | bytes 34568 | tf_op jit(solution)/shard_map/ppermute | solution.py:167
  455.4 11.1 %collective-permute-start.36 = (f32[1,2880]{1,0:T(1,128)S(1)}, f32[1,2880]{1,0:T(1,128)S(1)}, u32[]{:S(2)}, u32[]{:S(2)}) collective-permute-start(f32[1,2880]{1,0:T(1,128)S(1)} %get-tuple-element.880), channel_id=1, source_target_pairs={{0,2},{2,4},{4,6},{6,8},{8,10},{10,12},{12,14},{14,16},{16,18},{18... | collective-permute-start | bytes 34568 | tf_op jit(solution)/shard_map/ppermute | solution.py:167
  567.4 9.8 %collective-permute-start.67 = (f32[1,2880]{1,0:T(1,128)S(1)}, f32[1,2880]{1,0:T(1,128)S(1)}, u32[]{:S(2)}, u32[]{:S(2)}) collective-permute-start(f32[1,2880]{1,0:T(1,128)S(1)} %get-tuple-element.850), channel_id=1, source_target_pairs={{0,30},{2,0},{4,2},{6,4},{8,6},{10,8},{12,10},{14,12},{16,14},{18,... | collective-permute-start | bytes 34568 | tf_op jit(solution)/shard_map/ppermute | solution.py:167
  573.1 7.9 collective-permute-start.66
  573.1 8.5 %collective-permute-start.65 = (f32[1,2880]{1,0:T(1,128)S(1)}, f32[1,2880]{1,0:T(1,128)S(1)}, u32[]{:S(2)}, u32[]{:S(2)}) collective-permute-start(f32[1,2880]{1,0:T(1,128)S(1)} %get-tuple-element.852), channel_id=1, source_target_pairs={{0,26},{2,28},{4,30},{6,0},{8,2},{10,4},{12,6},{14,8},{16,10},{18,... | collective-permute-start | bytes 34568 | tf_op jit(solution)/shard_map/ppermute | solution.py:167
  573.7 8.9 %collective-permute-start.64 = (f32[1,2880]{1,0:T(1,128)S(1)}, f32[1,2880]{1,0:T(1,128)S(1)}, u32[]{:S(2)}, u32[]{:S(2)}) collective-permute-start(f32[1,2880]{1,0:T(1,128)S(1)} %get-tuple-element.853), channel_id=1, source_target_pairs={{0,24},{2,26},{4,28},{6,30},{8,0},{10,2},{12,4},{14,6},{16,8},{18,... | collective-permute-start | bytes 34568 | tf_op jit(solution)/shard_map/ppermute | solution.py:167
  575.7 10.6 %collective-permute-start.63 = (f32[1,2880]{1,0:T(1,128)S(1)}, f32[1,2880]{1,0:T(1,128)S(1)}, u32[]{:S(2)}, u32[]{:S(2)}) collective-permute-start(f32[1,2880]{1,0:T(1,128)S(1)} %get-tuple-element.854), channel_id=1, source_target_pairs={{0,22},{2,24},{4,26},{6,28},{8,30},{10,0},{12,2},{14,4},{16,6},{18... | collective-permute-start | bytes 34568 | tf_op jit(solution)/shard_map/ppermute | solution.py:167
  577.2 11.2 %collective-permute-start.62 = (f32[1,2880]{1,0:T(1,128)S(1)}, f32[1,2880]{1,0:T(1,128)S(1)}, u32[]{:S(2)}, u32[]{:S(2)}) collective-permute-start(f32[1,2880]{1,0:T(1,128)S(1)} %get-tuple-element.855), channel_id=1, source_target_pairs={{0,20},{2,22},{4,24},{6,26},{8,28},{10,30},{12,0},{14,2},{16,4},{1... | collective-permute-start | bytes 34568 | tf_op jit(solution)/shard_map/ppermute | solution.py:167
  581.0 9.0 %collective-permute-start.61 = (f32[1,2880]{1,0:T(1,128)S(1)}, f32[1,2880]{1,0:T(1,128)S(1)}, u32[]{:S(2)}, u32[]{:S(2)}) collective-permute-start(f32[1,2880]{1,0:T(1,128)S(1)} %get-tuple-element.856), channel_id=1, source_target_pairs={{0,18},{2,20},{4,22},{6,24},{8,26},{10,28},{12,30},{14,0},{16,2},{... | collective-permute-start | bytes 34568 | tf_op jit(solution)/shard_map/ppermute | solution.py:167
  581.6 8.8 %collective-permute-start.60 = (f32[1,2880]{1,0:T(1,128)S(1)}, f32[1,2880]{1,0:T(1,128)S(1)}, u32[]{:S(2)}, u32[]{:S(2)}) collective-permute-start(f32[1,2880]{1,0:T(1,128)S(1)} %get-tuple-element.857), channel_id=1, source_target_pairs={{0,16},{2,18},{4,20},{6,22},{8,24},{10,26},{12,28},{14,30},{16,0},... | collective-permute-start | bytes 34568 | tf_op jit(solution)/shard_map/ppermute | solution.py:167
  582.6 11.2 %collective-permute-start.59 = (f32[1,2880]{1,0:T(1,128)S(1)}, f32[1,2880]{1,0:T(1,128)S(1)}, u32[]{:S(2)}, u32[]{:S(2)}) collective-permute-start(f32[1,2880]{1,0:T(1,128)S(1)} %get-tuple-element.858), channel_id=1, source_target_pairs={{0,14},{2,16},{4,18},{6,20},{8,22},{10,24},{12,26},{14,28},{16,30}... | collective-permute-start | bytes 34568 | tf_op jit(solution)/shard_map/ppermute | solution.py:167
  586.4 10.3 %collective-permute-start.58 = (f32[1,2880]{1,0:T(1,128)S(1)}, f32[1,2880]{1,0:T(1,128)S(1)}, u32[]{:S(2)}, u32[]{:S(2)}) collective-permute-start(f32[1,2880]{1,0:T(1,128)S(1)} %get-tuple-element.859), channel_id=1, source_target_pairs={{0,12},{2,14},{4,16},{6,18},{8,20},{10,22},{12,24},{14,26},{16,28}... | collective-permute-start | bytes 34568 | tf_op jit(solution)/shard_map/ppermute | solution.py:167
  588.5 9.0 %collective-permute-start.57 = (f32[1,2880]{1,0:T(1,128)S(1)}, f32[1,2880]{1,0:T(1,128)S(1)}, u32[]{:S(2)}, u32[]{:S(2)}) collective-permute-start(f32[1,2880]{1,0:T(1,128)S(1)} %get-tuple-element.860), channel_id=1, source_target_pairs={{0,10},{2,12},{4,14},{6,16},{8,18},{10,20},{12,22},{14,24},{16,26}... | collective-permute-start | bytes 34568 | tf_op jit(solution)/shard_map/ppermute | solution.py:167
  590.0 7.6 collective-permute-start.56
  590.4 7.9 collective-permute-start.55
  596.7 7.4 collective-permute-start.53
  636.9 11.3 %all-to-all-start = ((bf16[16,8,512]{2,1,0:T(8,128)(2,1)}), bf16[16,8,512]{2,1,0:T(8,128)(2,1)S(1)}, u32[]{:S(2)}, u32[]{:S(2)}) async-start(bf16[16,8,512]{2,1,0:T(8,128)(2,1)} %bitcast_select_fusion), calls=%async_computation | async-start | bytes 262144 | tf_op jit(solution)/shard_map/all_to_all | solution.py:334
  640.4 154.7 %reduce-scatter.2.cloned.1.call-start = ((), (), s32[]{:S(2)}) async-start(), calls=%async_computation.3 | async-start | bytes 278528 | tf_op jit(solution)/shard_map/reduce_scatter | solution.py:349
  (425 other events, 3489.3 us)
Sparse Core Ops, SparseCore 0:
  720.9 74.1 reduce-scatter.1
